TPU v7x, 16 devices: a whole 2x2x2 slice. The times are simulated.
16 devices in a mesh: dp: 2 (over z), ep: 8 (over y, x, core).
Axes of the slice: x: 2, y: 2, z: 2, core: 2. Of those that a mesh axis runs over, the one named last changes fastest.
Arguments:
- hidden: bfloat16 [32768, 1024], P(('dp', 'ep'))
- grad_out: bfloat16 [32768, 1024], P(('dp', 'ep'))
- expert_ids: int32 [32768, 2], P(('dp', 'ep'))
- norm_gain: float32 [1024], replicated
- w_router: float32 [1024, 32], replicated
- w_gate: bfloat16 [32, 1024, 2816], P('ep')
- w_up: bfloat16 [32, 1024, 2816], P('ep')
- w_down: bfloat16 [32, 2816, 1024], P('ep')
Outputs:
- output 1: bfloat16 [32768, 1024], P(('dp', 'ep'))
- output 2: float32 [], replicated
- output 3: bfloat16 [32768, 1024], P(('dp', 'ep'))
- output 4: float32 [1024], replicated
- output 5: float32 [1024, 32], replicated
- output 6: bfloat16 [32, 1024, 2816], P('ep')
- output 7: bfloat16 [32, 1024, 2816], P('ep')
- output 8: bfloat16 [32, 2816, 1024], P('ep')
All inputs are finite; a program needn't handle non-finite values.
Results may differ from a plain program's by a relative error of at most 0.0146366.
Values are sent between devices in bfloat16 or wider.
A program may use at most 1 GiB of HBM per device.

v0:
```python
import jax
import jax.numpy as jnp
from jax import lax
from jax.sharding import PartitionSpec as P

EPS = 1e-6
AUX_COEF = 0.001


def route_tables(expert_ids, n_exp, capacity):
    flat_ids = expert_ids.reshape(-1)
    n_choice = flat_ids.shape[0]
    one_hot = (flat_ids[:, None] == jnp.arange(n_exp, dtype=jnp.int32)[None, :]).astype(jnp.int32)
    running = jnp.cumsum(one_hot, axis=0) - 1
    dest_rows = flat_ids * capacity + jnp.sum(running * one_hot, axis=1)
    slot_owner = jnp.full((n_exp * capacity,), n_choice, jnp.int32).at[dest_rows].set(jnp.arange(n_choice, dtype=jnp.int32))
    return dest_rows, slot_owner, jnp.sum(one_hot, axis=0)


def solution(mesh):
    n_dev = mesh.shape["dp"] * mesh.shape["ep"]
    all_axes = ("dp", "ep")

    def local_step(hidden, grad_out, expert_ids, norm_gain, w_router, w_gate, w_up, w_down):
        n_tok, width = hidden.shape
        n_exp = w_router.shape[1]
        capacity = 4 * n_tok // n_exp
        total_tok = n_tok * n_dev
        dest_rows, slot_owner, loads = route_tables(expert_ids, n_exp, capacity)
        choice_hot = (expert_ids[:, :, None] == jnp.arange(n_exp, dtype=jnp.int32)).astype(jnp.float32)

        x_f32 = hidden.astype(jnp.float32)
        inv_rms = lax.rsqrt(jnp.mean(x_f32 * x_f32, axis=-1, keepdims=True) + EPS)
        x_hat = x_f32 * inv_rms
        x_norm = (x_hat * norm_gain).astype(jnp.bfloat16)
        xn_f32 = x_norm.astype(jnp.float32)
        router_probs = jax.nn.softmax(jnp.dot(xn_f32, w_router, preferred_element_type=jnp.float32), axis=-1)
        gate_vals = jnp.sum(router_probs[:, None, :] * choice_hot, axis=-1)
        route_stats = lax.psum(jnp.concatenate([loads.astype(jnp.float32), jnp.sum(router_probs, axis=0)]), all_axes)
        load_frac = route_stats[:n_exp] / (2 * total_tok)
        aux_loss = AUX_COEF * n_exp * jnp.sum(load_frac * route_stats[n_exp:] / total_tok)

        send_rows = jnp.take(x_norm, slot_owner // 2, axis=0, mode="fill", fill_value=0).reshape(n_exp, capacity, width)
        recv_rows = lax.all_to_all(send_rows, "ep", 0, 1, tiled=True)
        h_gate = jnp.einsum("nrd,ndf->nrf", recv_rows, w_gate, preferred_element_type=jnp.float32).astype(jnp.bfloat16)
        h_up = jnp.einsum("nrd,ndf->nrf", recv_rows, w_up, preferred_element_type=jnp.float32).astype(jnp.bfloat16)
        gate_f32 = h_gate.astype(jnp.float32)
        up_f32 = h_up.astype(jnp.float32)
        sig_gate = jax.nn.sigmoid(gate_f32)
        silu_gate = gate_f32 * sig_gate
        act_rows = (silu_gate * up_f32).astype(jnp.bfloat16)
        exp_out = jnp.einsum("nrf,nfd->nrd", act_rows, w_down, preferred_element_type=jnp.float32).astype(jnp.bfloat16)
        back_rows = lax.all_to_all(exp_out, "ep", 1, 0, tiled=True).reshape(n_exp * capacity, width)
        picked = jnp.take(back_rows, dest_rows, axis=0).reshape(n_tok, 2, width)
        out_hidden = (x_f32 + jnp.sum(gate_vals[:, :, None] * picked, axis=1)).astype(jnp.bfloat16)

        dy_f32 = grad_out.astype(jnp.float32)
        d_gates = jnp.sum(dy_f32[:, None, :] * picked, axis=-1)
        d_picked = (dy_f32[:, None, :] * gate_vals[:, :, None]).astype(jnp.bfloat16).reshape(n_tok * 2, width)
        d_send = jnp.take(d_picked, slot_owner, axis=0, mode="fill", fill_value=0).reshape(n_exp, capacity, width)
        d_recv = lax.all_to_all(d_send, "ep", 0, 1, tiled=True)
        d_act = jnp.einsum("nrd,nfd->nrf", d_recv, w_down, preferred_element_type=jnp.float32)
        d_act = d_act.astype(jnp.bfloat16).astype(jnp.float32)
        g_down = jnp.einsum("nrf,nrd->nfd", act_rows, d_recv, preferred_element_type=jnp.float32)
        d_hup = (d_act * silu_gate).astype(jnp.bfloat16)
        d_hgate = (d_act * up_f32 * sig_gate * (1.0 + gate_f32 * (1.0 - sig_gate))).astype(jnp.bfloat16)
        g_gate = jnp.einsum("nrd,nrf->ndf", recv_rows, d_hgate, preferred_element_type=jnp.float32)
        g_up = jnp.einsum("nrd,nrf->ndf", recv_rows, d_hup, preferred_element_type=jnp.float32)
        d_rows = (jnp.einsum("nrf,ndf->nrd", d_hgate, w_gate, preferred_element_type=jnp.float32) + jnp.einsum("nrf,ndf->nrd", d_hup, w_up, preferred_element_type=jnp.float32)).astype(jnp.bfloat16)
        d_back = lax.all_to_all(d_rows, "ep", 1, 0, tiled=True).reshape(n_exp * capacity, width)
        d_xn_exp = jnp.take(d_back, dest_rows, axis=0).reshape(n_tok, 2, width)

        d_probs = jnp.sum(d_gates[:, :, None] * choice_hot, axis=1) + (AUX_COEF * n_exp / total_tok) * load_frac
        d_logits = router_probs * (d_probs - jnp.sum(router_probs * d_probs, axis=-1, keepdims=True))
        d_xnorm = jnp.einsum("te,de->td", d_logits, w_router) + d_xn_exp[:, 0].astype(jnp.float32) + d_xn_exp[:, 1].astype(jnp.float32)
        d_xnorm = d_xnorm.astype(jnp.bfloat16).astype(jnp.float32)
        value_a6 = d_xnorm * norm_gain
        grad_hidden = (inv_rms * (value_a6 - x_hat * jnp.mean(value_a6 * x_hat, axis=-1, keepdims=True)) + dy_f32).astype(jnp.bfloat16)
        small_grads = lax.psum((jnp.sum(d_xnorm * x_hat, axis=0), jnp.einsum("td,te->de", xn_f32, d_logits)), all_axes)
        big_grads = lax.psum((g_gate, g_up, g_down), "dp")
        return (out_hidden, aux_loss, grad_hidden, small_grads[0], small_grads[1], big_grads[0].astype(jnp.bfloat16), big_grads[1].astype(jnp.bfloat16), big_grads[2].astype(jnp.bfloat16))

    tok_spec = P(all_axes, None)
    w_spec = P("ep", None, None)
    return jax.shard_map(local_step, mesh=mesh, in_specs=(tok_spec, tok_spec, tok_spec, P(), P(), w_spec, w_spec, w_spec), out_specs=(tok_spec, P(), tok_spec, P(), P(), w_spec, w_spec, w_spec), check_vma=False)
```

profile of v0, /device:TPU:0, one launch (start us, length us, event | category | flops | bytes accessed | tf_op | source)
XLA Modules:
  0.0 4789.4 jit_solution(8715887236992921992)
XLA Ops:
  47.1 43.2 gather_fusion
  98.7 189.3 %all_to_all.66 = bf16[32,256,1024]{2,1,0:T(8,128)(2,1)S(1)} all-to-all(bf16[32,256,1024]{2,1,0:T(8,128)(2,1)S(1)} %broadcast_select_fusion.1), channel_id=1, replica_groups=mesh['dp'=2,'ep'=8] {'ep'}, dimensions={0} | all-to-all | bytes 33554432 | tf_op jit(solution)/shard_map/all_to_all | solution.py:44
  294.9 60.5 %convolution_convert_fusion.2 = bf16[4,2048,2816]{2,1,0:T(8,128)(2,1)} fusion(bf16[4,2048,1024]{2,1,0:T(8,128)(2,1)} %bitcast.71, bf16[4,1024,2816]{2,1,0:T(8,128)(2,1)} %param.15), kind=kOutput, calls=%fused_computation.22 | convolution fusion | flops 47267708928 | bytes 85983232 | tf_op jit(solution)/shard_map/nrd,ndf->nrf/dot_general | solution.py:45
  355.4 77.9 %fusion = (bf16[4,2048,2816]{2,1,0:T(8,128)(2,1)}, bf16[4,2048,2816]{2,1,0:T(8,128)(2,1)}) fusion(bf16[4,2048,2816]{2,1,0:T(8,128)(2,1)} %convolution_convert_fusion.2, bf16[4,2048,1024]{2,1,0:T(8,128)(2,1)} %bitcast.72, bf16[4,1024,2816]{2,1,0:T(8,128)(2,1)} %param.16), kind=kOutput, calls=%fused_computation.11 | convolution fusion | flops 47452258304 | bytes 178257920 | tf_op jit(solution)/shard_map/nrd,ndf->nrf/dot_general | solution.py:46
  433.4 57.0 %convolution_convert_fusion.3 = bf16[4,2048,1024]{2,1,0:T(8,128)(2,1)} fusion(bf16[4,2048,2816]{2,1,0:T(8,128)(2,1)} %get-tuple-element.34, bf16[4,2816,1024]{2,1,0:T(8,128)(2,1)} %param.17), kind=kOutput, calls=%fused_computation.29 | convolution fusion | flops 47253028864 | bytes 85983232 | tf_op jit(solution)/shard_map/nrf,nfd->nrd/dot_general | solution.py:52
  490.4 22.2 copy.58
  525.9 20.5 mul.174
  550.3 152.1 %all-to-all-done.1 = bf16[4,2048,1024]{2,0,1:T(4,128)(2,1)} async-done(((bf16[4,2048,1024]{2,0,1:T(4,128)(2,1)}), bf16[4,2048,1024]{2,0,1:T(4,128)(2,1)}, u32[]{:S(2)}, u32[]{:S(2)}) %all-to-all-start.1) | async-done | bytes 16777248 | tf_op jit(solution)/shard_map/all_to_all | solution.py:53
  719.5 28.8 gather_fusion.2
  768.9 44.9 gather_fusion.1
  833.9 208.5 %psum.42 = f32[64]{0:T(128)S(1)} all-reduce(f32[64]{0:T(128)S(1)} %pad_maximum_fusion), channel_id=1, replica_groups=mesh['dp'=2,'ep'=8] {'dp','ep'}, use_global_device_ids=true, to_apply=%region_11.13 | all-reduce | flops 64 | bytes 512 | tf_op jit(solution)/shard_map/psum | solution.py:39
  1062.1 103.2 %fusion.4 = (bf16[4,2048,2816]{2,1,0:T(8,128)(2,1)}, bf16[4,2048,2816]{2,1,0:T(8,128)(2,1)}) fusion(bf16[4,2048,2816]{2,1,0:T(8,128)(2,1)} %convolution_convert_fusion.2, bf16[4,2048,2816]{2,1,0:T(8,128)(2,1)} %get-tuple-element.35, bf16[4,2048,1024]{2,1,0:T(8,128)(2,1)} %bitcast.75, bf16[4,2816,1024]{2,1,0:T(8,128)(2,1)} %param.17), kind=kOutput, calls=%fused_computation.15 | convolution fusion | flops 47636807680 | bytes 224395264 | tf_op jit(solution)/shard_map/nrd,nfd->nrf/dot_general | solution.py:62
  1165.3 55.9 %fusion.38 = f32[4,2048,1024]{2,1,0:T(8,128)} fusion(bf16[4,2048,2816]{2,1,0:T(8,128)(2,1)} %get-tuple-element.21, bf16[4,1024,2816]{2,1,0:T(8,128)(2,1)} %param.15), kind=kOutput, calls=%fused_computation.100 | convolution fusion | flops 47244640256 | bytes 102760448 | tf_op jit(solution)/shard_map/nrf,ndf->nrd/dot_general | solution.py:69
  1221.2 60.5 %fusion.39 = f32[4,1024,2816]{2,1,0:T(8,128)} fusion(bf16[4,2048,1024]{2,1,0:T(8,128)(2,1)} %bitcast.73, bf16[4,2048,2816]{2,1,0:T(8,128)(2,1)} %get-tuple-element.21), kind=kOutput, calls=%fused_computation.101 | convolution fusion | flops 47244640256 | bytes 109051904 | tf_op jit(solution)/shard_map/nrd,nrf->ndf/dot_general | solution.py:67
  1281.8 59.2 %fusion.41 = f32[4,2816,1024]{2,1,0:T(8,128)} fusion(bf16[4,2048,2816]{2,1,0:T(8,128)(2,1)} %get-tuple-element.34, bf16[4,2048,1024]{2,1,0:T(8,128)(2,1)} %bitcast.76), kind=kOutput, calls=%fused_computation.103 | convolution fusion | flops 47244640256 | bytes 109051904 | tf_op jit(solution)/shard_map/nrf,nrd->nfd/dot_general | solution.py:64
  1341.0 60.6 %fusion.40 = f32[4,1024,2816]{2,1,0:T(8,128)} fusion(bf16[4,2048,1024]{2,1,0:T(8,128)(2,1)} %bitcast.74, bf16[4,2048,2816]{2,1,0:T(8,128)(2,1)} %get-tuple-element.20), kind=kOutput, calls=%fused_computation.102 | convolution fusion | flops 47244640256 | bytes 109051904 | tf_op jit(solution)/shard_map/nrd,nrf->ndf/dot_general | solution.py:68
  1401.6 56.7 %add_convert_fusion = bf16[4,2048,1024]{2,1,0:T(8,128)(2,1)} fusion(f32[4,2048,1024]{2,1,0:T(8,128)} %fusion.38, bf16[4,2048,2816]{2,1,0:T(8,128)(2,1)} %get-tuple-element.20, bf16[4,1024,2816]{2,1,0:T(8,128)(2,1)} %param.16), kind=kOutput, calls=%fused_computation.23 | convolution fusion | flops 47261417472 | bytes 119537664 | tf_op jit(solution)/shard_map/nrf,ndf->nrd/dot_general | solution.py:69
  1458.2 22.2 copy.63
  1486.1 3103.7 %all-reduce.5 = (bf16[4,1024,2816]{2,1,0:T(8,128)(2,1)}, bf16[4,1024,2816]{2,1,0:T(8,128)(2,1)}, bf16[4,2816,1024]{2,1,0:T(8,128)(2,1)}) all-reduce(f32[4,1024,2816]{2,1,0:T(8,128)} %fusion.39, f32[4,1024,2816]{2,1,0:T(8,128)} %fusion.40, f32[4,2816,1024]{2,1,0:T(8,128)} %fusion.41), channel_id=1, replica_groups=mesh['dp'=2,'ep'=8] {'dp'}, use_global_device_ids=true, to_apply=%region_20.22 | all-reduce | flops 34603008 | bytes 207618048 | tf_op jit(solution)/shard_map/psum | solution.py:80
  4607.1 28.8 gather_fusion.3
  4664.2 17.5 fusion.36
  4691.2 20.1 reshape.143
  4711.4 25.8 multiply_reduce_fusion.1
  4749.0 30.3 psum.43
  (114 shorter events, 223.0 us)
Async XLA Ops:
  7.2 539.3 %copy-start = (f32[1024,32]{0,1:T(8,128)S(1)}, f32[1024,32]{0,1:T(8,128)}, u32[]{:S(2)}) copy-start(f32[1024,32]{0,1:T(8,128)} %param.14) | copy-start | bytes 393220
  9.5 80.8 %copy-start.8 = (s32[4096]{0:T(1024)}, s32[4096]{0:T(1024)S(1)}, u32[]{:S(2)}) copy-start(s32[4096]{0:T(1024)S(1)} %eq.41) | copy-start | bytes 49156
  42.9 47.4 copy-start.16
  512.6 189.9 %all-to-all-start.1 = ((bf16[4,2048,1024]{2,0,1:T(4,128)(2,1)}), bf16[4,2048,1024]{2,0,1:T(4,128)(2,1)}, u32[]{:S(2)}, u32[]{:S(2)}) async-start(bf16[4,2048,1024]{2,0,1:T(4,128)(2,1)} %copy.58), calls=%async_computation.1 | async-start | bytes 33554432 | tf_op jit(solution)/shard_map/all_to_all | solution.py:53
  525.9 20.5 copy-start.22
  525.9 24.2 copy-start.9
  525.9 24.2 copy-start.11
  550.1 198.1 %copy-start.18 = (pred[4096]{0:T(1024)(128)(4,1)}, pred[4096]{0:T(1024)(128)(4,1)S(1)}, u32[]{:S(2)}) copy-start(pred[4096]{0:T(1024)(128)(4,1)S(1)} %compare_and_fusion.2) | copy-start | bytes 12292
  550.1 169.3 %copy-start.12 = (s32[4096]{0:T(1024)}, s32[4096]{0:T(1024)S(1)}, u32[]{:S(2)}) copy-start(s32[4096]{0:T(1024)S(1)} %broadcast_clamp_fusion.1) | copy-start | bytes 49156
  550.3 493.5 %copy-start.4 = (f32[2048,32]{0,1:T(8,128)}, f32[2048,32]{0,1:T(8,128)S(1)}, u32[]{:S(2)}) copy-start(f32[2048,32]{0,1:T(8,128)S(1)} %get-tuple-element.19) | copy-start | bytes 786436
  759.0 284.8 %copy-start.6 = (f32[2048,32]{0,1:T(8,128)}, f32[2048,32]{0,1:T(8,128)S(1)}, u32[]{:S(2)}) copy-start(f32[2048,32]{0,1:T(8,128)S(1)} %get-tuple-element.11) | copy-start | bytes 786436
  759.4 54.4 %copy-start.2 = (f32[2048,2]{1,0:T(8,128)}, f32[2048,2]{1,0:T(8,128)S(1)}, u32[]{:S(2)}) copy-start(f32[2048,2]{1,0:T(8,128)S(1)} %copy.53) | copy-start | bytes 49156
  827.9 220.3 %all-to-all-start.2 = ((bf16[32,256,1024]{2,1,0:T(8,128)(2,1)}), bf16[32,256,1024]{2,1,0:T(8,128)(2,1)}, u32[]{:S(2)}, u32[]{:S(2)}) async-start(bf16[32,256,1024]{2,1,0:T(8,128)(2,1)} %broadcast_select_fusion), calls=%async_computation.2 | async-start | bytes 33554432 | tf_op jit(solution)/shard_map/all_to_all | solution.py:61
  833.8 3945.6 %all-reduce.4.cloned.1.call-start = ((), (), s32[]{:S(2)}) async-start(), calls=%async_computation.4 | async-start | bytes 262144 | tf_op jit(solution)/shard_map/psum | solution.py:79
  1043.1 19.0 copy-start.24
  1480.4 3109.4 %all-to-all-start.3 = ((bf16[4,2048,1024]{2,0,1:T(4,128)(2,1)}), bf16[4,2048,1024]{2,0,1:T(4,128)(2,1)}, u32[]{:S(2)}, u32[]{:S(2)}) async-start(bf16[4,2048,1024]{2,0,1:T(4,128)(2,1)} %copy.63), calls=%async_computation.3 | async-start | bytes 33554432 | tf_op jit(solution)/shard_map/all_to_all | solution.py:70
  4607.1 28.8 copy-start.19
  4664.1 17.6 copy-start.5
  4664.1 17.6 copy-start.7
  4664.1 17.6 copy-start.17
  4664.2 17.6 copy-start.21
  4664.2 17.6 copy-start.23
  4664.2 17.6 copy-start.25
  4691.2 20.1 copy-start.3
  (7 other events, 63.9 us)
Sparse Core Ops, SparseCore 0:
  1048.3 65.8 all-reduce.3
where the time goes:
time: 4800 us; the launch traced here: 4790 us
  blocking collectives  3530 us (74%)
  matrix products  608 us (13%)
  local copies, waits for them, and re-layouts  348 us (7%)
  waiting for transfers between devices  152 us (3%)
  other arithmetic  115 us (2%)
    psum x1, blocking collectives, local_step(): big_grads = lax.psum((g_gate, g_up, g_down), 'dp')  3100 us
    psum x1, blocking collectives, local_step(): lax.psum(jnp.concatenate([loads.astype(jnp.float32), jnp.sum(router_probs...  208 us
    all_to_all x1, blocking collectives, local_step(): recv_rows = lax.all_to_all(send_rows, 'ep', 0, 1, tiled=True)  189 us
    all_to_all x1, waiting for transfers between devices, local_step(): lax.all_to_all(exp_out, 'ep', 1, 0, tiled=True)  152 us
    dot_general x1, matrix products, local_step(): jnp.einsum('nrd,nfd->nrf', d_recv, w_down, preferred_element_type=jnp.flo...  103 us
  transfers between devices with their start and end apart: 4, of which 1 were waited for; matrix products, arithmetic and copies ran while one was open for 13% of the time, Pallas kernels for 0%

commit v1 on v0

v1 whole, which is shorter than its diff:
```python
import functools

import jax
import jax.numpy as jnp
from jax import lax
from jax.experimental import pallas as pl
from jax.experimental.pallas import tpu as pltpu
from jax.sharding import PartitionSpec as P

EPS = 1e-6
AUX_COEF = 0.001
ROW_TILE = 256
GROUP_TILE = 512
CHUNK_ALIGN = 16
COL = 256
VMEM = 66_000_000
F32 = jnp.float32
BF16 = jnp.bfloat16


def route_tables(expert_ids, n_exp, capacity):
    flat_ids = expert_ids.reshape(-1)
    n_choice = flat_ids.shape[0]
    one_hot = (flat_ids[:, None] == jnp.arange(n_exp, dtype=jnp.int32)[None, :]).astype(jnp.int32)
    running = jnp.cumsum(one_hot, axis=0) - 1
    dest_rows = flat_ids * capacity + jnp.sum(running * one_hot, axis=1)
    slot_owner = jnp.full((n_exp * capacity,), n_choice, jnp.int32).at[dest_rows].set(jnp.arange(n_choice, dtype=jnp.int32))
    return dest_rows, slot_owner


def mm(a, b):
    return jnp.dot(a, b, preferred_element_type=F32)


def mm_t(a, b):
    return lax.dot_general(a, b, (((1,), (1,)), ((), ())), preferred_element_type=F32)


def fwd_kernel(tile_row, tile_exp, count, x_ref, wg_ref, wu_ref, wd_ref, hg_ref, hu_ref, o_ref, act_s):
    @pl.when(pl.program_id(0) < count[0])
    def _():
        ff, width = wd_ref.shape[1:]
        for j in range(ff // COL):
            cols = slice(j * COL, (j + 1) * COL)
            hg = mm(x_ref[...], wg_ref[0, :, cols]).astype(BF16)
            hu = mm(x_ref[...], wu_ref[0, :, cols]).astype(BF16)
            hg_ref[:, cols] = hg
            hu_ref[:, cols] = hu
            gate = hg.astype(F32)
            act_s[:, cols] = (gate * jax.nn.sigmoid(gate) * hu.astype(F32)).astype(BF16)
        for j in range(width // COL):
            cols = slice(j * COL, (j + 1) * COL)
            o_ref[:, cols] = mm(act_s[...], wd_ref[0, :, cols]).astype(BF16)


def gate_grads(gate, up, d_act):
    sig = jax.nn.sigmoid(gate)
    silu = gate * sig
    act = (silu * up).astype(BF16)
    d_hup = (d_act * silu).astype(BF16)
    d_hgate = (d_act * up * sig * (1.0 + gate * (1.0 - sig))).astype(BF16)
    return act, d_hgate, d_hup


def bwd_kernel(tile_row, tile_exp, count, hg_ref, hu_ref, dy_ref, w_ref, wg_ref, wu_ref, wd_ref, act_ref, dhg_ref, dhu_ref, dx_ref, do_s):
    @pl.when(pl.program_id(0) < count[0])
    def _():
        ff, width = wd_ref.shape[1:]
        do_s[...] = (dy_ref[...].astype(F32) * w_ref[...]).astype(BF16)
        for j in range(ff // COL):
            cols = slice(j * COL, (j + 1) * COL)
            d_act = mm_t(do_s[...], wd_ref[0, cols, :]).astype(BF16).astype(F32)
            act, dhg, dhu = gate_grads(hg_ref[:, cols].astype(F32), hu_ref[:, cols].astype(F32), d_act)
            act_ref[:, cols] = act
            dhg_ref[:, cols] = dhg
            dhu_ref[:, cols] = dhu
        for j in range(width // COL):
            cols = slice(j * COL, (j + 1) * COL)
            dx_ref[:, cols] = (mm_t(dhg_ref[...], wg_ref[0, cols, :]) + mm_t(dhu_ref[...], wu_ref[0, cols, :])).astype(BF16)


def both_kernel(tile_row, tile_exp, count, x_ref, dy_ref, w_ref, wg_ref, wu_ref, wd_ref, a_in, b_in, c_in, act_ref, dhg_ref, dhu_ref, do_s):
    del a_in, b_in, c_in

    @pl.when(pl.program_id(0) < count[0])
    def _():
        ff = wd_ref.shape[1]
        do_s[...] = (dy_ref[...].astype(F32) * w_ref[...]).astype(BF16)
        for j in range(ff // COL):
            cols = slice(j * COL, (j + 1) * COL)
            gate = mm(x_ref[...], wg_ref[0, :, cols]).astype(BF16).astype(F32)
            up = mm(x_ref[...], wu_ref[0, :, cols]).astype(BF16).astype(F32)
            d_act = mm_t(do_s[...], wd_ref[0, cols, :]).astype(BF16).astype(F32)
            act, dhg, dhu = gate_grads(gate, up, d_act)
            act_ref[:, cols] = act
            dhg_ref[:, cols] = dhg
            dhu_ref[:, cols] = dhu


def outer_kernel(scaled_rhs, tile_row, tile_exp, half, count, l_ref, r_ref, *refs):
    if scaled_rhs:
        w_ref, out_ref, acc, left_t, right_s = refs
    else:
        out_ref, acc, left_t = refs
    i = pl.program_id(0)
    n = count[0]
    last_step = pl.num_programs(0) - 1
    me = tile_exp[i]
    first = jnp.logical_or(i == 0, tile_exp[jnp.maximum(i - 1, 0)] != me)
    last = jnp.logical_or(i == n - 1, tile_exp[jnp.minimum(i + 1, last_step)] != me)
    live = i < n

    def add(rows):
        left_t[:, :rows] = l_ref[:rows, :].T
        if scaled_rhs:
            right_s[:rows, :] = (r_ref[:rows, :].astype(F32) * w_ref[:rows, :]).astype(BF16)
            right = right_s
        else:
            right = r_ref

        @pl.loop(0, acc.shape[1] // COL)
        def _(j):
            cols = pl.ds(pl.multiple_of(j * COL, COL), COL)
            acc[:, cols] += mm(left_t[:, :rows], right[:rows, cols])

    @pl.when(jnp.logical_and(live, first))
    def _():
        acc[...] = jnp.zeros_like(acc)

    @pl.when(jnp.logical_and(live, half[i] == 0))
    def _():
        add(GROUP_TILE)

    @pl.when(jnp.logical_and(live, half[i] == 1))
    def _():
        add(GROUP_TILE // 2)

    @pl.when(jnp.logical_and(live, last))
    def _():
        out_ref[0] = acc[...].astype(BF16)


def spread_kernel(n_chunk, rows, starts, src, dst, buf, in_sem, out_sem):
    def fetch(i):
        at = pl.multiple_of(starts[i], CHUNK_ALIGN)
        return pltpu.make_async_copy(src.at[pl.ds(at, rows), :], buf.at[i], in_sem.at[i])

    def put(i):
        return pltpu.make_async_copy(buf.at[i], dst.at[i], out_sem.at[i])

    for i in range(n_chunk):
        fetch(i).start()
    for i in range(n_chunk):
        fetch(i).wait()
        put(i).start()
    for i in range(n_chunk):
        put(i).wait()


def params():
    return pltpu.CompilerParams(dimension_semantics=("arbitrary",), vmem_limit_bytes=VMEM)


def cost(flops, nbytes):
    return pl.CostEstimate(flops=int(flops), bytes_accessed=int(nbytes), transcendentals=0)


def row_spec(cols, base=0):
    return pl.BlockSpec((ROW_TILE, cols), lambda i, r, e, c: (r[i] + base, 0))


def exp_spec(a, b):
    return pl.BlockSpec((1, a, b), lambda i, r, e, c: (e[i], 0, 0))


def solution(mesh):
    n_dp, n_ep = mesh.shape["dp"], mesh.shape["ep"]
    n_dev = n_dp * n_ep
    all_axes = ("dp", "ep")

    def local_step(hidden, grad_out, expert_ids, norm_gain, w_router, w_gate, w_up, w_down):
        n_tok, width = hidden.shape
        n_exp = w_router.shape[1]
        n_loc, _, ff = w_gate.shape
        capacity = 4 * n_tok // n_exp
        n_choice = 2 * n_tok
        total_tok = n_tok * n_dev
        half_rows = n_loc * n_ep * capacity
        my_dp, my_ep = lax.axis_index("dp"), lax.axis_index("ep")

        x_f32 = hidden.astype(F32)
        inv_rms = lax.rsqrt(jnp.mean(x_f32 * x_f32, axis=-1, keepdims=True) + EPS)
        x_hat = x_f32 * inv_rms
        x_norm = (x_hat * norm_gain).astype(BF16)
        xn_all = lax.all_gather(x_norm, all_axes, tiled=True)
        dest_rows, slot_owner = route_tables(expert_ids, n_exp, capacity)
        slots = lax.all_gather(slot_owner.reshape(n_exp, capacity), all_axes)
        dy_all = lax.all_gather(grad_out, all_axes, tiled=True)

        choice_hot = (expert_ids[:, :, None] == jnp.arange(n_exp, dtype=jnp.int32)).astype(F32)
        xn_f32 = x_norm.astype(F32)
        router_probs = jax.nn.softmax(jnp.dot(xn_f32, w_router, preferred_element_type=F32), axis=-1)
        gate_vals = jnp.sum(router_probs[:, None, :] * choice_hot, axis=-1)
        gate_slots = jnp.zeros((n_exp * capacity,), F32).at[dest_rows].set(gate_vals.reshape(-1))
        gates = lax.all_gather(gate_slots.reshape(n_exp, capacity), all_axes)
        xn_all, gates = lax.optimization_barrier((xn_all, gates))
        load_frac = jnp.sum((slots < n_choice).astype(F32), axis=(0, 2)) / (2 * total_tok)

        def mine(table):
            table = lax.dynamic_slice(table, (0, n_loc * my_ep, 0), (n_dev, n_loc, capacity))
            planes = table.reshape(n_dp, n_ep, n_loc, capacity)
            planes = jnp.where(my_dp == 0, planes, planes[::-1])
            return planes.transpose(0, 2, 1, 3)

        src_dev = (jnp.arange(n_dp)[:, None] + my_dp) % n_dp * n_ep + jnp.arange(n_ep)[None, :]
        my_slots = mine(slots)
        used = my_slots < n_choice
        load = jnp.sum(used.astype(jnp.int32), axis=-1)
        token_of = jnp.where(used, my_slots // 2 + src_dev[:, None, :, None].astype(jnp.int32) * n_tok, 0)
        room = (load + CHUNK_ALIGN - 1) // CHUNK_ALIGN * CHUNK_ALIGN
        chunk_at = jnp.cumsum(room, axis=2) - room
        group_rows = jnp.sum(room, axis=2)
        n_small = (group_rows + ROW_TILE - 1) // ROW_TILE
        n_small = jnp.maximum(n_small, jnp.array([[1], [0]], jnp.int32))
        n_big = (n_small + 1) // 2
        big_at = jnp.cumsum(n_big, axis=1) - n_big

        row = jnp.arange(half_rows, dtype=jnp.int32)
        exp_hot = (row // GROUP_TILE >= big_at[:, :, None]).astype(jnp.int32)
        exp_hot = exp_hot - jnp.concatenate([exp_hot[:, 1:], jnp.zeros_like(exp_hot[:, :1])], axis=1)
        within = row - jnp.sum(exp_hot * big_at[:, :, None], axis=1) * GROUP_TILE
        exp_of = jnp.sum(exp_hot * jnp.arange(n_loc, dtype=jnp.int32)[:, None], axis=1)
        at_row = jnp.sum(exp_hot[:, :, None, :] * chunk_at[:, :, :, None], axis=1)
        load_row = jnp.sum(exp_hot[:, :, None, :] * load[:, :, :, None], axis=1)
        src_hot = (within[:, None, :] >= at_row).astype(jnp.int32)
        src_hot = src_hot - jnp.concatenate([src_hot[:, 1:], jnp.zeros_like(src_hot[:, :1])], axis=1)
        slot = within - jnp.sum(src_hot * at_row, axis=1)
        live = slot < jnp.sum(src_hot * load_row, axis=1)
        src_of = jnp.sum(src_hot * jnp.arange(n_ep, dtype=jnp.int32)[:, None], axis=1)
        half_of = jnp.arange(n_dp, dtype=jnp.int32)[:, None]
        flat = (((half_of * n_loc + exp_of) * n_ep + src_of) * capacity + jnp.minimum(slot, capacity - 1)).reshape(-1)
        row_token = jnp.take(token_of.reshape(-1), flat, mode="clip")
        row_gate = jnp.where(live.reshape(-1), jnp.take(mine(gates).reshape(-1), flat, mode="clip"), 0.0)[:, None]

        x_rows = jnp.take(xn_all, row_token, axis=0, mode="clip")
        dy_rows = jnp.take(dy_all, row_token, axis=0, mode="clip")

        n_step = half_rows // ROW_TILE

        def small_tiles(h):
            ends = jnp.cumsum(n_small[h])
            i = jnp.minimum(jnp.arange(n_step, dtype=jnp.int32), jnp.maximum(ends[-1] - 1, 0))
            e = jnp.minimum(jnp.sum((i[None, :] >= ends[:, None]).astype(jnp.int32), axis=0), n_loc - 1)
            pick = (e[None, :] == jnp.arange(n_loc, dtype=jnp.int32)[:, None]).astype(jnp.int32)
            first = jnp.sum(pick * (2 * big_at[h] - ends + n_small[h])[:, None], axis=0)
            return first + i, e, ends[-1:]

        def big_tiles():
            n = n_big.T.reshape(-1)
            ends = jnp.cumsum(n)
            at = (big_at + jnp.arange(n_dp, dtype=jnp.int32)[:, None] * (half_rows // GROUP_TILE)).T.reshape(-1)
            i = jnp.minimum(jnp.arange(n_step, dtype=jnp.int32), ends[-1] - 1)
            q = jnp.sum((i[None, :] >= ends[:, None]).astype(jnp.int32), axis=0)
            pick = (q[None, :] == jnp.arange(n_dp * n_loc, dtype=jnp.int32)[:, None]).astype(jnp.int32)
            j = i - jnp.sum(pick * (ends - n)[:, None], axis=0)
            small = jnp.sum(pick * n_small.T.reshape(-1)[:, None], axis=0)
            return jnp.sum(pick * at[:, None], axis=0) + j, q // n_dp, (small - 2 * j < 2).astype(jnp.int32), ends[-1:]

        own_tiles, other_tiles, sum_tiles = small_tiles(0), small_tiles(1), big_tiles()
        all_rows = n_dp * half_rows
        wide = jax.ShapeDtypeStruct((all_rows, ff), BF16)
        mat_flops = half_rows * width * ff
        w_bytes = 2 * n_loc * width * ff

        h_gate, h_up, out_rows = pl.pallas_call(
            fwd_kernel,
            out_shape=(jax.ShapeDtypeStruct((half_rows, ff), BF16),) * 2 + (jax.ShapeDtypeStruct((half_rows + capacity, width), BF16),),
            grid_spec=pltpu.PrefetchScalarGridSpec(
                num_scalar_prefetch=3,
                grid=(n_step,),
                in_specs=[row_spec(width), exp_spec(width, ff), exp_spec(width, ff), exp_spec(ff, width)],
                out_specs=[row_spec(ff), row_spec(ff), row_spec(width)],
                scratch_shapes=[pltpu.VMEM((ROW_TILE, ff), BF16)],
            ),
            compiler_params=params(),
            cost_estimate=cost(3 * mat_flops, 3 * w_bytes + half_rows * (2 * ff + 2 * width)),
            name="expert_fwd",
        )(*own_tiles, x_rows, w_gate, w_up, w_down)

        n_chunk = n_ep * n_loc
        starts = (big_at[0][:, None] * GROUP_TILE + chunk_at[0]).T.reshape(-1)

        def send_back(rows, name):
            packed = pl.pallas_call(
                functools.partial(spread_kernel, n_chunk, capacity),
                out_shape=jax.ShapeDtypeStruct((n_chunk, capacity, width), BF16),
                grid_spec=pltpu.PrefetchScalarGridSpec(
                    num_scalar_prefetch=1,
                    grid=(),
                    in_specs=[pl.BlockSpec(memory_space=pl.ANY)],
                    out_specs=pl.BlockSpec(memory_space=pl.ANY),
                    scratch_shapes=[pltpu.VMEM((n_chunk, capacity, width), BF16), pltpu.SemaphoreType.DMA((n_chunk,)), pltpu.SemaphoreType.DMA((n_chunk,))],
                ),
                compiler_params=pltpu.CompilerParams(vmem_limit_bytes=VMEM),
                cost_estimate=cost(1e9, 4 * half_rows * width),
                name=name,
            )(starts, rows)
            return lax.all_to_all(packed, "ep", 0, 0, tiled=True).reshape(n_exp * capacity, width)

        back_rows = send_back(out_rows, "pack_out")

        act_rows, d_hgate, d_hup, dx_rows = pl.pallas_call(
            bwd_kernel,
            out_shape=(wide, wide, wide, jax.ShapeDtypeStruct((half_rows + capacity, width), BF16)),
            grid_spec=pltpu.PrefetchScalarGridSpec(
                num_scalar_prefetch=3,
                grid=(n_step,),
                in_specs=[row_spec(ff), row_spec(ff), row_spec(width), row_spec(1), exp_spec(width, ff), exp_spec(width, ff), exp_spec(ff, width)],
                out_specs=[row_spec(ff), row_spec(ff), row_spec(ff), row_spec(width)],
                scratch_shapes=[pltpu.VMEM((ROW_TILE, width), BF16)],
            ),
            compiler_params=params(),
            cost_estimate=cost(3 * mat_flops, 3 * w_bytes + half_rows * (5 * ff + 2 * width)),
            name="expert_bwd",
        )(*own_tiles, h_gate, h_up, dy_rows, row_gate, w_gate, w_up, w_down)

        d_back = send_back(dx_rows, "pack_dx")

        any_spec = pl.BlockSpec(memory_space=pl.ANY)
        act_rows, d_hgate, d_hup = pl.pallas_call(
            both_kernel,
            out_shape=(wide, wide, wide),
            grid_spec=pltpu.PrefetchScalarGridSpec(
                num_scalar_prefetch=3,
                grid=(n_step,),
                in_specs=[row_spec(width, n_step), row_spec(width, n_step), row_spec(1, n_step), exp_spec(width, ff), exp_spec(width, ff), exp_spec(ff, width), any_spec, any_spec, any_spec],
                out_specs=[row_spec(ff, n_step)] * 3,
                scratch_shapes=[pltpu.VMEM((ROW_TILE, width), BF16)],
            ),
            input_output_aliases={9: 0, 10: 1, 11: 2},
            compiler_params=params(),
            cost_estimate=cost(3 * mat_flops, 3 * w_bytes + half_rows * (3 * ff + 2 * width)),
            name="expert_other",
        )(*other_tiles, x_rows, dy_rows, row_gate, w_gate, w_up, w_down, act_rows, d_hgate, d_hup)

        def outer(left, right, scale, name):
            a, b = left.shape[1], right.shape[1]

            def spec(cols):
                return pl.BlockSpec((GROUP_TILE, cols), lambda i, r, e, h, c: (r[i], 0))

            scaled = scale is not None
            return pl.pallas_call(
                functools.partial(outer_kernel, scaled),
                out_shape=jax.ShapeDtypeStruct((n_loc, a, b), BF16),
                grid_spec=pltpu.PrefetchScalarGridSpec(
                    num_scalar_prefetch=4,
                    grid=(n_step,),
                    in_specs=[spec(a), spec(b)] + ([spec(1)] if scaled else []),
                    out_specs=pl.BlockSpec((1, a, b), lambda i, r, e, h, c: (e[i], 0, 0)),
                    scratch_shapes=[pltpu.VMEM((a, b), F32), pltpu.VMEM((a, GROUP_TILE), BF16)] + ([pltpu.VMEM((GROUP_TILE, b), BF16)] if scaled else []),
                ),
                compiler_params=params(),
                cost_estimate=cost(2 * mat_flops, w_bytes + all_rows * (a + b)),
                name=name,
            )(*sum_tiles, left, right, *([scale] if scaled else []))

        g_gate = outer(x_rows, d_hgate, None, "grad_gate")
        g_up = outer(x_rows, d_hup, None, "grad_up")
        g_down = outer(act_rows, dy_rows, row_gate, "grad_down")

        dest = dest_rows.reshape(n_tok, 2)
        picked = [jnp.take(back_rows, dest[:, j], axis=0, mode="clip").astype(F32) for j in range(2)]
        out_hidden = (x_f32 + (gate_vals[:, :1] * picked[0] + gate_vals[:, 1:] * picked[1])).astype(BF16)
        dy_f32 = grad_out.astype(F32)
        d_gates = [jnp.sum(dy_f32 * p, axis=-1, keepdims=True) for p in picked]
        d_probs = d_gates[0] * choice_hot[:, 0] + d_gates[1] * choice_hot[:, 1] + (AUX_COEF * n_exp / total_tok) * load_frac
        d_logits = router_probs * (d_probs - jnp.sum(router_probs * d_probs, axis=-1, keepdims=True))
        d_taken = [jnp.take(d_back, dest[:, j], axis=0, mode="clip").astype(F32) for j in range(2)]
        d_xnorm = jnp.einsum("te,de->td", d_logits, w_router) + d_taken[0] + d_taken[1]
        d_xnorm = d_xnorm.astype(BF16).astype(F32)
        scaled = d_xnorm * norm_gain
        grad_hidden = (inv_rms * (scaled - x_hat * jnp.mean(scaled * x_hat, axis=-1, keepdims=True)) + dy_f32).astype(BF16)
        prob_sum, g_gain, g_router = lax.psum((jnp.sum(router_probs, axis=0), jnp.sum(d_xnorm * x_hat, axis=0), jnp.einsum("td,te->de", xn_f32, d_logits)), all_axes)
        aux_loss = AUX_COEF * n_exp * jnp.sum(load_frac * prob_sum / total_tok)
        return (out_hidden, aux_loss, grad_hidden, g_gain, g_router, g_gate, g_up, g_down)

    tok_spec = P(all_axes, None)
    w_spec = P("ep", None, None)
    return jax.shard_map(local_step, mesh=mesh, in_specs=(tok_spec, tok_spec, tok_spec, P(), P(), w_spec, w_spec, w_spec), out_specs=(tok_spec, P(), tok_spec, P(), P(), w_spec, w_spec, w_spec), check_vma=False)
```

time: 4800 us -> 2490 us (0.52)
  blocking collectives: 3530 us -> 120 us
  local copies, waits for them, and re-layouts: 348 us -> 1450 us
  Pallas kernels: 0 us -> 687 us
  matrix products: 608 us -> 13 us
  waiting for transfers between devices: 152 us -> 80.7 us
  other arithmetic: 115 us -> 54.6 us
    psum x3 -> x1, blocking collectives: 3340 us -> 88.3 us  [local_step(): lax.psum((jnp.sum(router_probs, axis=0), jnp.sum(d_xnorm * x_hat, axis=0)...]
    gather x4 -> x9, local copies, waits for them, and re-layouts: 146 us -> 1400 us  [the longest x1 570 us: local_step(): dy_rows = jnp.take(dy_all, row_token, axis=0, mode='clip')]
    pallas_call x0 -> x8, Pallas kernels: none -> 687 us  [the longest x3 310 us: outer(): pl.pallas_call(functools.partial(outer_kernel, scaled), out_shape=jax.Sha...]
    dot_general x11 -> x2, matrix products: 605 us -> 11.5 us  [the longest x1 7.98 us: local_step(): jnp.einsum('te,de->td', d_logits, w_router) + d_taken[0] + d_taken[1]]
    all_to_all x1 -> x0, blocking collectives: 189 us -> none  [local_step(): recv_rows = lax.all_to_all(send_rows, 'ep', 0, 1, tiled=True)]
    all_to_all x3 -> x2, waiting for transfers between devices: 152 us -> 0.01 us  [send_back(): lax.all_to_all(packed, 'ep', 0, 0, tiled=True)]
    convert_element_type x3 -> x0, local copies, waits for them, and re-layouts: 64.5 us -> none  [the longest x1 22.2 us: local_step(): (jnp.einsum('nrf,ndf->nrd', d_hgate, w_gate, preferred_element_type=jnp.f...]
    all_gather x0 -> x2, waiting for transfers between devices: none -> 63 us  [the longest x1 63 us: local_step(): xn_all = lax.all_gather(x_norm, all_axes, tiled=True)]
  transfers between devices with their start and end apart: 4 -> 5, of which waited for: 1 -> 2; matrix products, arithmetic and copies ran while one was open for 13% -> 60% of each run, Pallas kernels for 0% -> 28%
where the time goes in v1:
time: 2490 us; the launch traced here: 2450 us
  local copies, waits for them, and re-layouts  1450 us (58%)
  Pallas kernels  687 us (28%)
  blocking collectives  120 us (5%)
  waiting for transfers between devices  80.7 us (3%)
  other arithmetic  54.6 us (2%)
    gather x1, local copies, waits for them, and re-layouts, local_step(): dy_rows = jnp.take(dy_all, row_token, axis=0, mode='clip')  570 us
    gather x1, local copies, waits for them, and re-layouts, local_step(): x_rows = jnp.take(xn_all, row_token, axis=0, mode='clip')  569 us
    pallas_call x3, Pallas kernels, outer(): pl.pallas_call(functools.partial(outer_kernel, scaled), out_shape=jax.Sha...  310 us
    pallas_call x1, Pallas kernels, local_step(): pl.pallas_call(bwd_kernel, out_shape=(wide, wide, wide, jax.ShapeDtypeStr...  125 us
    pallas_call x1, Pallas kernels, local_step(): pl.pallas_call(both_kernel, out_shape=(wide, wide, wide), grid_spec=pltpu...  122 us
    pallas_call x1, Pallas kernels, local_step(): pl.pallas_call(fwd_kernel, out_shape=(jax.ShapeDtypeStruct((half_rows, ff...  104 us
    gather x2, local copies, waits for them, and re-layouts, local_step(): jnp.take(mine(gates).reshape(-1), flat, mode='clip')  95.4 us
    gather x1, local copies, waits for them, and re-layouts, local_step(): row_token = jnp.take(token_of.reshape(-1), flat, mode='clip')  90.5 us
  transfers between devices with their start and end apart: 5, of which 2 were waited for; matrix products, arithmetic and copies ran while one was open for 60% of the time, Pallas kernels for 28%

profile of v1, /device:TPU:0, one launch (start us, length us, event | category | flops | bytes accessed | tf_op | source)
XLA Modules:
  0.0 2448.2 jit_solution(840632179279744513)
XLA Ops:
  30.8 15.5 scatter_custom_fusion
  46.4 17.3 all_gather.12
  76.8 15.5 scatter_custom_fusion.1
  93.1 90.5 %gather_fusion = s32[16384]{0:T(1024)S(1)} fusion(s32[16384]{0:T(1024)S(1)} %bitcast.111, s32[16384]{0:T(1024)S(1)} %broadcast_clamp_fusion.1), kind=kCustom, calls=%fused_computation | custom fusion | bytes 196608 | tf_op jit(solution)/shard_map/jit(_take)/gather | solution.py:242
  185.5 14.7 all_gather.14
  200.9 63.0 %all-gather.3.cloned.1.call-done = bf16[32768,1024]{1,0:T(8,128)(2,1)} async-done(((bf16[2048,1024]{1,0:T(8,128)(2,1)}), bf16[32768,1024]{1,0:T(8,128)(2,1)}) %all-gather.3.cloned.1.call-update) | async-done | bytes 67108880 | tf_op jit(solution)/shard_map/all_gather | solution.py:195
  264.0 569.0 %gather_fusion.1 = bf16[16384,1024]{1,0:T(8,128)(2,1)} fusion(bf16[32768,1024]{1,0:T(8,128)(2,1)} %all-gather.3.cloned.1.call-done, s32[16384]{0:T(1024)S(1)} %broadcast_clamp_fusion), kind=kCustom, calls=%fused_computation.1 | custom fusion | bytes 67174400 | tf_op jit(solution)/shard_map/jit(_take)/gather | solution.py:245
  833.0 103.6 %expert_fwd.1 = (bf16[8192,2816]{1,0:T(8,128)(2,1)}, bf16[8192,2816]{1,0:T(8,128)(2,1)}, bf16[8448,1024]{1,0:T(8,128)(2,1)}) custom-call(s32[32]{0:T(128)} %fusion.55.tile_row, s32[32]{0:T(128)} %copy-done.41, s32[1]{0:T(128)} %bitcast.10.count, bf16[16384,1024]{1,0:T(8,128)(2,1)} %gather_fusion.1, bf16[4,1024,2816]{2,1,0:T(8,128)(2,1)} %wg_ref.5, ...), custom_call_target="tpu_custom_call" | custom-call | flops 70866960384 | bytes 132120576 | tf_op jit(solution)/shard_map/expert_fwd/pallas_call | solution.py:275
  936.6 13.1 pack_out.1
  974.4 90.5 %gather_fusion.5 = f32[16384]{0:T(1024)S(1)} fusion(f32[16384]{0:T(1024)S(1)} %bitcast.112, s32[16384]{0:T(1024)S(1)} %copy-done.10), kind=kCustom, calls=%fused_computation.5 | custom fusion | bytes 196608 | tf_op jit(solution)/shard_map/jit(_take)/gather | solution.py:243
  1069.9 569.9 %gather_fusion.4 = bf16[16384,1024]{1,0:T(8,128)(2,1)} fusion(bf16[32768,1024]{1,0:T(8,128)(2,1)} %all-gather.5.cloned.1.call-done, s32[16384]{0:T(1024)S(1)} %broadcast_clamp_fusion), kind=kCustom, calls=%fused_computation.4 | custom fusion | bytes 67174400 | tf_op jit(solution)/shard_map/jit(_take)/gather | solution.py:246
  1645.7 124.9 %expert_bwd.1 = (bf16[16384,2816]{1,0:T(8,128)(2,1)}, bf16[16384,2816]{1,0:T(8,128)(2,1)}, bf16[16384,2816]{1,0:T(8,128)(2,1)}, bf16[8448,1024]{1,0:T(8,128)(2,1)}) custom-call(s32[32]{0:T(128)} %fusion.55.tile_row, s32[32]{0:T(128)} %copy-done.41, s32[1]{0:T(128)} %bitcast.10.count, bf16[8192,2816]{1,0:T(8,128)(2,1)} %get-tuple-element.22.hg_ref, ...), custom_call_target="tpu_custom_call" | custom-call | flops 70866960384 | bytes 201326592 | tf_op jit(solution)/shard_map/expert_bwd/pallas_call | solution.py:312
  1770.6 13.1 pack_dx.1
  1783.7 13.1 all-to-all-start.1
  1797.0 122.1 %expert_other.1 = (bf16[16384,2816]{1,0:T(8,128)(2,1)}, bf16[16384,2816]{1,0:T(8,128)(2,1)}, bf16[16384,2816]{1,0:T(8,128)(2,1)}) custom-call(s32[32]{0:T(128)} %fusion.56.tile_row, s32[32]{0:T(128)} %copy-done.40, s32[1]{0:T(128)} %bitcast.26.count, bf16[16384,1024]{1,0:T(8,128)(2,1)} %gather_fusion.1, ...), custom_call_target="tpu_custom_call", output_to_operand_aliasing={{0}: (9, {}), {1}: (10, {}), {2}: (11, {})} | custom-call | flops 70866960384 | bytes 155189248 | tf_op jit(solution)/shard_map/expert_other/pallas_call | solution.py:330
  1919.1 97.1 %grad_down.1 = bf16[4,2816,1024]{2,1,0:T(8,128)(2,1)} custom-call(s32[32]{0:T(128)} %get-tuple-element.81.tile_row, s32[32]{0:T(128)} %get-tuple-element.80.tile_exp, s32[32]{0:T(128)} %compare_convert_fusion.2.half, s32[1]{0:T(128)} %bitcast.23.count, bf16[16384,2816]{1,0:T(8,128)(2,1)} %get-tuple-element.31.l_ref, bf16[16384,1024]{1,0:T(8,128)(2,1)} %gather_fusion.4, ...), custom_call_target="tpu_custom_call" | custom-call | flops 47244640256 | bytes 85983232 | tf_op jit(solution)/shard_map/grad_down/pallas_call | solution.py:353
  2016.3 106.2 %grad_gate.1 = bf16[4,1024,2816]{2,1,0:T(8,128)(2,1)} custom-call(s32[32]{0:T(128)} %get-tuple-element.81.tile_row, s32[32]{0:T(128)} %get-tuple-element.80.tile_exp, s32[32]{0:T(128)} %compare_convert_fusion.2.half, s32[1]{0:T(128)} %bitcast.23.count, bf16[16384,1024]{1,0:T(8,128)(2,1)} %gather_fusion.1, bf16[16384,2816]{1,0:T(8,128)(2,1)} %get-tuple-element.29.r_ref), custom_call_target="tpu_custom_call" | custom-call | flops 47244640256 | bytes 85983232 | tf_op jit(solution)/shard_map/grad_gate/pallas_call | solution.py:353
  2122.5 106.4 %grad_up.1 = bf16[4,1024,2816]{2,1,0:T(8,128)(2,1)} custom-call(s32[32]{0:T(128)} %get-tuple-element.81.tile_row, s32[32]{0:T(128)} %get-tuple-element.80.tile_exp, s32[32]{0:T(128)} %compare_convert_fusion.2.half, s32[1]{0:T(128)} %bitcast.23.count, bf16[16384,1024]{1,0:T(8,128)(2,1)} %gather_fusion.1, bf16[16384,2816]{1,0:T(8,128)(2,1)} %get-tuple-element.30.r_ref), custom_call_target="tpu_custom_call" | custom-call | flops 47244640256 | bytes 85983232 | tf_op jit(solution)/shard_map/grad_up/pallas_call | solution.py:353
  2228.9 18.9 gather_fusion.3
  2247.8 18.9 gather_fusion.2
  2266.7 19.1 gather_fusion.7
  2285.9 18.9 gather_fusion.6
  2324.7 88.3 %all-reduce.2 = (f32[32]{0:T(128)S(1)}, f32[1024]{0:T(1024)}) all-reduce(f32[32]{0:T(128)S(1)} %get-tuple-element.42, f32[1024]{0:T(1024)S(1)} %get-tuple-element.32), channel_id=1, replica_groups=mesh['dp'=2,'ep'=8] {'dp','ep'}, use_global_device_ids=true, to_apply=%region_23.24 | all-reduce | flops 1056 | bytes 8448 | tf_op jit(solution)/shard_map/psum | solution.py:384
  2421.6 17.0 all-reduce.5.cloned.1.call-done
  (208 shorter events, 102.8 us)
Async XLA Ops:
  7.2 63.2 %copy-start = (f32[1024,32]{0,1:T(8,128)S(1)}, f32[1024,32]{0,1:T(8,128)}, u32[]{:S(2)}) copy-start(f32[1024,32]{0,1:T(8,128)} %param.13) | copy-start | bytes 393220
  7.2 256.8 %all-gather.3.cloned.1.call-start = ((), (), s32[]{:S(2)}) async-start(), calls=%async_computation.2 | async-start | bytes 71303168 | tf_op jit(solution)/shard_map/all_gather | solution.py:195
  15.1 1054.7 %all-gather.5.cloned.1.call-start = ((), (), s32[]{:S(2)}) async-start(), calls=%async_computation.3 | async-start | bytes 71303168 | tf_op jit(solution)/shard_map/all_gather | solution.py:198
  15.9 50.0 %copy-start.31 = (s32[2]{0:T(128)S(1)}, s32[2]{0:T(128)}, u32[]{:S(2)}) copy-start(s32[2]{0:T(128)} %constant.202) | copy-start | bytes 28
  67.1 117.2 %copy-start.37 = (s32[4,1]{0,1:T(1,128)}, s32[4,1]{0,1:T(1,128)S(1)}, u32[]{:S(2)}) copy-start(s32[4,1]{0,1:T(1,128)S(1)} %broadcast_in_dim.41) | copy-start | bytes 52
  76.0 107.6 %copy-start.13 = (f32[2048,2]{0,1:T(2,128)}, f32[2048,2]{0,1:T(2,128)S(1)}, u32[]{:S(2)}) copy-start(f32[2048,2]{0,1:T(2,128)S(1)} %select_reduce_fusion) | copy-start | bytes 49156
  93.1 90.6 %copy-start.9 = (s32[16384]{0:T(1024)}, s32[16384]{0:T(1024)S(1)}, u32[]{:S(2)}) copy-start(s32[16384]{0:T(1024)S(1)} %broadcast_clamp_fusion.1) | copy-start | bytes 196612
  184.2 648.8 %copy-start.41 = (s32[32]{0:T(128)}, s32[32]{0:T(128)S(1)}, u32[]{:S(2)}) copy-start(s32[32]{0:T(128)S(1)} %broadcast_minimum_fusion.1.tile_exp) | copy-start | bytes 388
  949.7 12.1 copy-start.17
  949.7 16.6 copy-start.39
  949.8 18.0 copy-start.2
  949.8 21.7 copy-start.14
  949.8 22.3 copy-start.12
  949.8 24.6 %copy-start.10 = (s32[16384]{0:T(1024)S(1)}, s32[16384]{0:T(1024)}, u32[]{:S(2)}) copy-start(s32[16384]{0:T(1024)} %copy-done.9) | copy-start | bytes 196612
  949.8 833.9 %all-to-all-start = ((bf16[32,256,1024]{2,1,0:T(8,128)(2,1)}), bf16[32,256,1024]{2,1,0:T(8,128)(2,1)}, u32[]{:S(2)}, u32[]{:S(2)}) async-start(bf16[32,256,1024]{2,1,0:T(8,128)(2,1)} %pack_out.1), calls=%async_computation | async-start | bytes 33554432 | tf_op jit(solution)/shard_map/all_to_all | solution.py:308
  966.3 98.7 %copy-start.40 = (s32[32]{0:T(128)}, s32[32]{0:T(128)S(1)}, u32[]{:S(2)}) copy-start(s32[32]{0:T(128)S(1)} %broadcast_minimum_fusion.tile_exp) | copy-start | bytes 388
  967.8 97.2 %copy-start.34 = (f32[32]{0:T(128)}, f32[32]{0:T(128)S(1)}, u32[]{:S(2)}) copy-start(f32[32]{0:T(128)S(1)} %convert_reduce_fusion) | copy-start | bytes 388
  1783.7 482.9 %all-to-all-start.1 = ((bf16[32,256,1024]{2,1,0:T(8,128)(2,1)}), bf16[32,256,1024]{2,1,0:T(8,128)(2,1)}, u32[]{:S(2)}, u32[]{:S(2)}) async-start(bf16[32,256,1024]{2,1,0:T(8,128)(2,1)} %pack_dx.1), calls=%async_computation.1 | async-start | bytes 33554432 | tf_op jit(solution)/shard_map/all_to_all | solution.py:308
  1796.8 641.8 %all-reduce.5.cloned.1.call-start = ((), (), s32[]{:S(2)}) async-start(), calls=%async_computation.4 | async-start | bytes 262144 | tf_op jit(solution)/shard_map/psum | solution.py:384
  2122.5 106.4 %copy-start.23 = (s32[2048]{0:T(1024)S(1)}, s32[2048]{0:T(1024)}, u32[]{:S(2)}) copy-start(s32[2048]{0:T(1024)} %get-tuple-element.78) | copy-start | bytes 24580
  2228.9 18.9 copy-start.22
  2285.8 18.9 copy-start.24
  2285.8 18.9 copy-start.25
  2304.9 11.9 copy-start.21
  (23 other events, 148.9 us)
Sparse Core Ops, SparseCore 0:
  15.3 248.6 all-gather.2
  266.2 242.0 all-gather.4
  2316.8 121.6 all-reduce.4
